TPU v7x, 128 devices: a whole 4x4x4 slice. The times are simulated.
128 devices in a mesh: cp: 32 (over y, z, core), ep: 4 (over x).
Axes of the slice: x: 4, y: 4, z: 4, core: 2. Of those that a mesh axis runs over, the one named last changes fastest.
Arguments:
- residual: bfloat16 [4096, 6144], P('cp'), may hold values from -90 to 90
- queries: bfloat16 [4096, 3072], P('cp', 'ep'), may hold values from -256 to 256
- key_proj: bfloat16 [4096, 512], P('cp', 'ep'), may hold values from -8 to 8
- value_proj: bfloat16 [4096, 512], P('cp', 'ep'), may hold values from -12 to 12
- out_weight: bfloat16 [3072, 6144], P('ep'), may hold values from -0.109375 to 0.109375
- norm_gain: float32 [6144], replicated, may hold values from 0.1 to 1.9
- doc_ids: int32 [4096], replicated, may hold values from 0 to 11, never falling along the last dimension, each value on 1 to 1024 neighbouring positions
- block_order: int32 [32], replicated, may hold values from 0 to 31, each once
- expert_ids: int32 [4096, 2], P('cp'), may hold values from 0 to 7, as said below
- route_logits: float32 [4096, 2], P('cp'), may hold values from -12 to 12
- gate_weight: bfloat16 [4, 6144, 8192], P('ep', None, 'cp'), may hold values from -0.078125 to 0.078125
- up_weight: bfloat16 [4, 6144, 8192], P('ep', None, 'cp'), may hold values from -0.078125 to 0.078125
- down_weight: bfloat16 [4, 8192, 6144], P('ep', 'cp'), may hold values from -0.0625 to 0.0625
Outputs:
- hidden_state: bfloat16 [4096, 6144], P('cp', 'ep')
- expert_mix: bfloat16 [4096, 6144], P('cp', 'ep')
Inputs may be any that keep to these rules, and one draw needn't show every extreme that they name: `expert_ids`: each row names two different experts; within the 128 rows of one cp index no expert is named by more than 40 rows. `doc_ids`: document numbers never fall along the sequence. `block_order`: each block number appears once.
All inputs are finite; a program needn't handle non-finite values.
Results may differ from a plain program's by a relative error of at most 0.02.
Values may be sent and summed in bfloat16 or wider, within the bound.
No kernel may reach another device: no remote copies, remote signals or barrier semaphores. Data moves between devices by JAX's collectives and lax.ppermute only.
A program may use at most 128 MiB of HBM per device.

v0:
```python
import math
import jax
import jax.numpy as jnp
from jax import lax
from jax.sharding import PartitionSpec as P

HD = 128
CAP = 40
EPS = 1e-05
NEG = -1e30


def in_one_piece(arrays, axis, dim, along):
    both = jnp.concatenate(arrays, axis=along)
    out, at, outs = (lax.all_gather(both, axis, axis=dim, tiled=True), 0, [])
    for a in arrays:
        outs.append(lax.slice_in_dim(out, at, at + a.shape[along], axis=along))
        at += a.shape[along]
    return tuple(outs)


def cut_along(shard, dim, size):
    before, after = (shard.shape[:dim], shard.shape[dim + 1 :])
    return jnp.moveaxis(shard.reshape(*before, size, -1, *after), dim, 0)


def summed_on_arrival(shard, axis, dim):
    blocks = cut_along(shard, dim, lax.axis_size(axis))
    arrived = lax.all_to_all(blocks, axis, split_axis=0, concat_axis=0, tiled=True)
    return arrived.astype(jnp.float32).sum(axis=0)


def expert_hidden(rows_in, gate_weight, up_weight):
    gated = jnp.dot(rows_in, gate_weight[0], preferred_element_type=jnp.float32)
    lifted = jnp.dot(rows_in, up_weight[0], preferred_element_type=jnp.float32)
    return (jax.nn.silu(gated) * lifted).astype(jnp.bfloat16)


def local(
    residual,
    queries,
    key_proj,
    value_proj,
    out_weight,
    norm_gain,
    doc_ids,
    block_order,
    expert_ids,
    route_logits,
    gate_weight,
    up_weight,
    down_weight,
):
    tokens = residual.shape[0]
    kv_heads = key_proj.shape[1] // HD
    group_size = queries.shape[1] // HD // kv_heads
    score_scale = 1.0 / math.sqrt(HD)
    cp_rank = lax.axis_index("cp")
    ep_rank = lax.axis_index("ep")
    ep_count = lax.axis_size("ep")
    placed = lax.dynamic_slice_in_dim(block_order, cp_rank, 1)[0]
    own_pos = placed * tokens + jnp.arange(tokens, dtype=jnp.int32)
    own_docs = lax.dynamic_slice_in_dim(doc_ids, placed * tokens, tokens)
    query_grid = queries.reshape(tokens, kv_heads, group_size, HD)

    def attend_all(running, shard_piece):
        piece_keys, piece_values, piece_docs, piece_pos = shard_piece
        allowed = (piece_docs[None, :] == own_docs[:, None]) & (
            piece_pos[None, :] <= own_pos[:, None]
        )
        piece_width = piece_keys.shape[0]
        running_max, row_total, weighted = running[0]
        query_rows = query_grid[:, 0].reshape(tokens * group_size, HD)
        scores = lax.dot_general(
            query_rows, piece_keys, (((1,), (1,)), ((), ())), preferred_element_type=jnp.float32
        )
        scores = scores.reshape(tokens, group_size, piece_width) * score_scale
        scores = jnp.where(allowed[:, None, :], scores, NEG)
        new_max = jnp.maximum(running_max, jnp.max(scores, axis=2))
        weights = jnp.where(allowed[:, None, :], jnp.exp(scores - new_max[:, :, None]), 0.0)
        row_total = jnp.sum(weights, axis=2)
        value_mix = jnp.dot(
            weights.astype(jnp.bfloat16).reshape(tokens * group_size, piece_width),
            piece_values,
            preferred_element_type=jnp.float32,
        )
        weighted = value_mix.reshape(tokens, group_size, HD)
        updated = [(new_max, row_total, weighted)]
        return tuple(updated)

    start_state = tuple(
        (
            (
                jnp.full((tokens, group_size), NEG, jnp.float32),
                jnp.zeros((tokens, group_size), jnp.float32),
                jnp.zeros((tokens, group_size, HD), jnp.float32),
            )
            for kv_index in range(kv_heads)
        )
    )
    shard_piece = (
        *in_one_piece((key_proj, value_proj), "cp", 0, 1),
        lax.all_gather(own_docs, "cp", axis=0, tiled=True),
        lax.all_gather(own_pos, "cp", axis=0, tiled=True),
    )
    needed = jnp.any(
        (shard_piece[2][None, :] == own_docs[:, None])
        & (shard_piece[3][None, :] <= own_pos[:, None])
    )
    attn_state = lax.cond(
        needed, lambda inner: attend_all(inner, shard_piece), lambda inner: inner, start_state
    )
    attended = jnp.concatenate(
        [
            (weighted / row_total[:, :, None]).reshape(tokens, group_size * HD)
            for running_max, row_total, weighted in attn_state
        ],
        axis=1,
    ).astype(jnp.bfloat16)
    projected = jnp.dot(attended, out_weight, preferred_element_type=jnp.float32)
    quarter_width = residual.shape[1] // ep_count
    summed = lax.psum(projected.astype(jnp.bfloat16), "ep").astype(jnp.float32)
    hidden_full = (residual.astype(jnp.float32) + summed).astype(jnp.bfloat16)
    hidden_state = lax.dynamic_slice_in_dim(hidden_full, ep_rank * quarter_width, quarter_width, 1)
    values_wide = hidden_full.astype(jnp.float32)
    mean_square = jnp.mean(values_wide * values_wide, axis=1, keepdims=True)
    normed = (values_wide * lax.rsqrt(mean_square + EPS) * norm_gain).astype(jnp.bfloat16)
    logit_gap = route_logits[:, 1] - route_logits[:, 0]
    first_share = 1.0 / (1.0 + jnp.exp(logit_gap))
    second_share = 1.0 / (1.0 + jnp.exp(-logit_gap))
    slot_ids = jnp.arange(CAP, dtype=jnp.int32)
    expert = ep_rank * gate_weight.shape[0]
    is_member = ((expert_ids[:, 0] == expert) | (expert_ids[:, 1] == expert)).astype(jnp.int32)
    slot_index = jnp.cumsum(is_member) - is_member
    selector = ((slot_index[None, :] == slot_ids[:, None]) & (is_member[None, :] == 1)).astype(
        jnp.bfloat16
    )
    route_share = jnp.where(expert_ids[:, 0] == expert, first_share, 0.0) + jnp.where(
        expert_ids[:, 1] == expert, second_share, 0.0
    )
    slot_index, selector, route_share = (slot_index, selector, route_share)
    packed = jnp.dot(selector, normed, preferred_element_type=jnp.float32).astype(jnp.bfloat16)
    hidden = expert_hidden(lax.all_gather(packed, "cp", axis=0, tiled=True), gate_weight, up_weight)
    rows_in = lax.slice_in_dim(hidden, 0, CAP * lax.axis_size("cp"), axis=0)
    expert_sum = lax.psum_scatter(
        jnp.dot(rows_in, down_weight[0], preferred_element_type=jnp.float32).astype(jnp.bfloat16),
        "cp",
        scatter_dimension=0,
        tiled=True,
    ).astype(jnp.float32)
    gathered = jnp.take(expert_sum, jnp.minimum(slot_index, CAP - 1), axis=0)
    contribution = gathered * route_share[:, None]
    mixed_share = summed_on_arrival(contribution.astype(jnp.bfloat16), "ep", 1)
    return (hidden_state, mixed_share.astype(jnp.bfloat16))


def solution(mesh):
    return jax.shard_map(
        local,
        mesh=mesh,
        in_specs=(
            P("cp", None),
            P("cp", "ep"),
            P("cp", "ep"),
            P("cp", "ep"),
            P("ep", None),
            P(),
            P(),
            P(),
            P("cp", None),
            P("cp", None),
            P("ep", None, "cp"),
            P("ep", None, "cp"),
            P("ep", "cp", None),
        ),
        out_specs=(P("cp", "ep"), P("cp", "ep")),
        check_vma=False,
    )
```

profile of v0, /device:TPU:0, one launch (start us, length us, event | category | flops | bytes accessed | tf_op | source)
XLA Modules:
  0.0 387.8 jit_solution(3691068288422893904)
XLA Ops:
  7.2 1.6 pad_maximum_fusion
  11.5 23.1 %all-gather.1 = s32[32,1,128]{2,1,0:T(1,128)S(1)} all-gather(s32[1,1,128]{2,1,0:T(1,128)S(1)} %fusion.40), channel_id=1, replica_groups=mesh['cp'=32,'ep'=4] {'cp'}, dimensions={0}, use_global_device_ids=true | all-gather | bytes 16896 | tf_op jit(solution)/shard_map/all_gather | solution.py:104
  35.4 20.4 %all-gather = s32[32,1,128]{2,1,0:T(1,128)S(1)} all-gather(s32[1,1,128]{2,1,0:T(1,128)S(1)} %dynamic-slice_bitcast_fusion), channel_id=1, replica_groups=mesh['cp'=32,'ep'=4] {'cp'}, dimensions={0}, use_global_device_ids=true | all-gather | bytes 16896 | tf_op jit(solution)/shard_map/all_gather | solution.py:103
  58.4 15.5 %conditional.1 = (f32[128,6]{0,1:T(8,128)}, f32[128,6,128]{0,2,1:T(8,128)S(1)}) conditional(s32[]{:T(128)} %convert_element_type.64, () %tuple.16, (s32[4096]{0:T(1024)}, s32[128]{0:T(128)}, s32[4096]{0:T(1024)S(1)}, s32[128]{0:T(128)}, bf16[128,768]{1,0:T(8,128)(2,1)}, /*index=5*/bf16[4096,256]{1,0:T(8,128)(2,1)}) %tuple.42), branch_computations={%region_1.0_spmd, %region_2.5_spmd} | conditional | flops 1653079296 | bytes 53465160 | solution.py:110
  58.4 2.0 compare_and_fusion
  61.5 3.9 %fusion = (f32[128,6]{0,1:T(8,128)S(1)}, f32[128,6,4096]{2,0,1:T(8,128)S(1)}) fusion(pred[128,4096]{1,0:T(8,128)(4,1)} %compare_and_fusion, bf16[128,6,128]{0,2,1:T(8,128)(2,1)S(1)} %bitcast.58, bf16[4096,256]{1,0:T(8,128)(2,1)} %get-tuple-element.20), kind=kOutput, calls=%fused_computation.3 | convolution fusion | flops 814742784 | bytes 14355456 | tf_op jit(solution)/shard_map/cond/branch_1_fun/dot_general | solution.py:74
  65.5 4.7 %fusion.2 = f32[128,6]{0,1:T(8,128)} fusion(f32[128,6,4096]{2,0,1:T(8,128)S(1)} %get-tuple-element.61, f32[128,6]{0,1:T(8,128)S(1)} %broadcast_maximum_fusion, pred[128,4096]{1,0:T(8,128)(4,1)S(1)} %copy-done.1), kind=kLoop, calls=%fused_computation.5 | loop fusion | flops 15727872 | bytes 13113344 | tf_op jit(solution)/shard_map/cond/branch_1_fun/reduce_sum | solution.py:81
  70.2 3.6 fusion.3
  74.6 6.3 %convolution_convert_fusion.1 = bf16[128,6144]{1,0:T(8,128)(2,1)} fusion(bf16[128,768]{0,1:T(8,128)(2,1)S(1)} %bitcast.57, bf16[768,6144]{1,0:T(8,128)(2,1)} %param.19), kind=kOutput, calls=%fused_computation.19 | convolution fusion | flops 1208745984 | bytes 11206656 | tf_op jit(solution)/shard_map/dot_general | solution.py:120
  81.3 49.7 %all-reduce.2.cloned.1.call-done = bf16[128,6144]{1,0:T(8,128)(2,1)} async-done(((bf16[128,6144]{1,0:T(8,128)(2,1)}), bf16[128,6144]{1,0:T(8,128)(2,1)}) %all-reduce.2.cloned.1.call-update) | async-done | bytes 1572880 | tf_op jit(solution)/shard_map/psum | solution.py:122
  131.0 2.6 fusion.14
  136.4 70.2 %all-gather.7.cloned.1.call-done = bf16[1280,6144]{1,0:T(8,128)(2,1)} async-done(((bf16[40,6144]{1,0:T(8,128)(2,1)}), bf16[1280,6144]{1,0:T(8,128)(2,1)}) %all-gather.7.cloned.1.call-update) | async-done | bytes 15728656 | tf_op jit(solution)/shard_map/all_gather | solution.py:143
  206.7 9.4 %fusion.22 = f32[1280,256]{1,0:T(8,128)S(1)} fusion(bf16[1280,6144]{1,0:T(8,128)(2,1)} %all-gather.7.cloned.1.call-done, bf16[1,6144,256]{2,1,0:T(8,128)(2,1)} %param.25), kind=kOutput, calls=%fused_computation.32 | convolution fusion | flops 4026531840 | bytes 20185088 | tf_op jit(solution)/shard_map/dot_general | solution.py:34
  216.1 1.5 copy-done.9
  218.4 4.6 %fusion.27 = bf16[1280,256]{1,0:T(8,128)(2,1)S(1)} fusion(bf16[1280,6144]{1,0:T(8,128)(2,1)S(1)} %copy-done.9, bf16[1,6144,256]{2,1,0:T(8,128)(2,1)S(1)} %copy-done.10, f32[1280,256]{1,0:T(8,128)S(1)} %fusion.22), kind=kOutput, calls=%fused_computation.36 | convolution fusion | flops 4028497920 | bytes 20840448 | tf_op jit(solution)/shard_map/dot_general | solution.py:35
  223.1 7.8 %convolution_convert_fusion = bf16[1280,6144]{1,0:T(8,128)(2,1)} fusion(bf16[1280,256]{1,0:T(8,128)(2,1)S(1)} %fusion.27, bf16[1,256,6144]{2,1,0:T(8,128)(2,1)S(1)} %copy-done), kind=kOutput, calls=%fused_computation.18 | convolution fusion | flops 4034396160 | bytes 19529728 | tf_op jit(solution)/shard_map/dot_general | solution.py:146
  231.6 111.8 %reduce-scatter.2.cloned.1.call-done = bf16[40,6144]{1,0:T(8,128)(2,1)} async-done(((bf16[1280,6144]{1,0:T(8,128)(2,1)}), bf16[40,6144]{1,0:T(8,128)(2,1)}) %reduce-scatter.2.cloned.1.call-update) | async-done | bytes 491536 | tf_op jit(solution)/shard_map/reduce_scatter | solution.py:145
  343.4 2.1 convert_element_type.76
  345.4 5.7 %gather_fusion = f32[128,6144]{1,0:T(8,128)} fusion(f32[40,6144]{1,0:T(8,128)} %convert_element_type.76, s32[1024]{0:T(1024)S(1)} %pad_clamp_fusion), kind=kCustom, calls=%fused_computation | custom fusion | bytes 6291968 | tf_op jit(solution)/shard_map/jit(_take)/gather | solution.py:151
  351.1 3.5 fusion.30
  354.6 4.3 %all-to-all-start = ((bf16[4,128,1536]{2,1,0:T(8,128)(2,1)}), bf16[4,128,1536]{2,1,0:T(8,128)(2,1)}, u32[]{:S(2)}, u32[]{:S(2)}) async-start(bf16[4,128,1536]{2,1,0:T(8,128)(2,1)} %fusion.30), calls=%async_computation.1 | async-start | bytes 3145728 | tf_op jit(solution)/shard_map/all_to_all | solution.py:29
  359.0 1.8 constant_dynamic-slice_fusion
  360.7 18.0 %all-to-all-done = bf16[4,128,1536]{2,1,0:T(8,128)(2,1)} async-done(((bf16[4,128,1536]{2,1,0:T(8,128)(2,1)}), bf16[4,128,1536]{2,1,0:T(8,128)(2,1)}, u32[]{:S(2)}, u32[]{:S(2)}) %all-to-all-start) | async-done | bytes 1572896 | tf_op jit(solution)/shard_map/all_to_all | solution.py:29
  378.8 2.5 reduce_sum.31
  (51 shorter events, 11.4 us)
Async XLA Ops:
  7.2 215.9 %copy-start = (bf16[1,256,6144]{2,1,0:T(8,128)(2,1)S(1)}, bf16[1,256,6144]{2,1,0:T(8,128)(2,1)}, u32[]{:S(2)}) copy-start(bf16[1,256,6144]{2,1,0:T(8,128)(2,1)} %param.27) | copy-start | bytes 9437188
  7.2 51.2 %all-gather.5.cloned.1.call-start = ((), (), s32[]{:S(2)}) async-start(), calls=%async_computation.2 | async-start | bytes 2162688 | tf_op jit(solution)/shard_map/all_gather | solution.py:15
  8.8 122.2 %all-reduce.2.cloned.1.call-start = ((), (), s32[]{:S(2)}) async-start(), calls=%async_computation.3 | async-start | bytes 3145728 | tf_op jit(solution)/shard_map/psum | solution.py:122
  11.5 44.2 %copy-start.6 = (s32[128]{0:T(128)}, s32[128]{0:T(128)S(1)}, u32[]{:S(2)}) copy-start(s32[128]{0:T(128)S(1)} %dynamic_slice.10) | copy-start | bytes 1540
  55.8 0.6 copy-start.4
  55.8 0.6 copy-start.7
  61.5 4.0 %copy-start.1 = (pred[128,4096]{1,0:T(8,128)(4,1)S(1)}, pred[128,4096]{1,0:T(8,128)(4,1)}, u32[]{:S(2)}) copy-start(pred[128,4096]{1,0:T(8,128)(4,1)} %compare_and_fusion) | copy-start | bytes 1572868 | tf_op jit(solution)/shard_map/cond
  65.4 4.8 %copy-start.3 = (bf16[4096,256]{1,0:T(8,128)(2,1)S(1)}, bf16[4096,256]{1,0:T(8,128)(2,1)}, u32[]{:S(2)}) copy-start(bf16[4096,256]{1,0:T(8,128)(2,1)} %get-tuple-element.20) | copy-start | bytes 6291460 | tf_op jit(solution)/shard_map/cond
  74.5 6.4 %copy-start.5 = (s32[128,2]{0,1:T(2,128)S(1)}, s32[128,2]{0,1:T(2,128)}, u32[]{:S(2)}) copy-start(s32[128,2]{0,1:T(2,128)} %param.23) | copy-start | bytes 3076
  80.8 53.9 %copy-start.11 = (f32[6144]{0:T(1024)S(1)}, f32[6144]{0:T(1024)}, u32[]{:S(2)}) copy-start(f32[6144]{0:T(1024)} %param.20) | copy-start | bytes 73732
  80.9 125.8 %all-gather.7.cloned.1.call-start = ((), (), s32[]{:S(2)}) async-start(), calls=%async_computation.4 | async-start | bytes 16220160 | tf_op jit(solution)/shard_map/all_gather | solution.py:143
  133.6 1.1 copy-start.2
  136.2 207.2 %reduce-scatter.2.cloned.1.call-start = ((), (), s32[]{:S(2)}) async-start(), calls=%async_computation.5 | async-start | bytes 16220160 | tf_op jit(solution)/shard_map/reduce_scatter | solution.py:145
  206.7 10.8 %copy-start.9 = (bf16[1280,6144]{1,0:T(8,128)(2,1)S(1)}, bf16[1280,6144]{1,0:T(8,128)(2,1)}, u32[]{:S(2)}) copy-start(bf16[1280,6144]{1,0:T(8,128)(2,1)} %all-gather.7.cloned.1.call-done) | copy-start | bytes 47185924
  206.7 11.7 %copy-start.10 = (bf16[1,6144,256]{2,1,0:T(8,128)(2,1)S(1)}, bf16[1,6144,256]{2,1,0:T(8,128)(2,1)}, u32[]{:S(2)}) copy-start(bf16[1,6144,256]{2,1,0:T(8,128)(2,1)} %param.26) | copy-start | bytes 9437188
  230.9 0.7 copy-start.8
  354.6 24.2 %all-to-all-start = ((bf16[4,128,1536]{2,1,0:T(8,128)(2,1)}), bf16[4,128,1536]{2,1,0:T(8,128)(2,1)}, u32[]{:S(2)}, u32[]{:S(2)}) async-start(bf16[4,128,1536]{2,1,0:T(8,128)(2,1)} %fusion.30), calls=%async_computation.1 | async-start | bytes 3145728 | tf_op jit(solution)/shard_map/all_to_all | solution.py:29
Sparse Core Ops, SparseCore 0:
  10.8 46.2 all-gather.4
  81.0 49.9 all-reduce.1
  136.3 70.3 all-gather.6
  231.0 112.3 reduce-scatter.1
where the time goes:
time: 388 us
  waiting for transfers between devices  250 us (64%)
  blocking collectives  43.5 us (11%)
  matrix products  37 us (10%)
  other arithmetic  21.3 us (5%)
  local copies, waits for them, and re-layouts  16.2 us (4%)
  between operations  15.2 us (4%)
  starting transfers between devices  4.68 us (1%)
    reduce_scatter x1, waiting for transfers between devices, local(): lax.psum_scatter(jnp.dot(rows_in, down_weight[0], preferred_element_type=...  112 us
    all_gather x1, waiting for transfers between devices, local(): lax.all_gather(packed, 'cp', axis=0, tiled=True)  70.2 us
    psum x1, waiting for transfers between devices, local(): summed = lax.psum(projected.astype(jnp.bfloat16), 'ep').astype(jnp.float32)  49.7 us
    all_gather x1, blocking collectives, local(): lax.all_gather(own_pos, 'cp', axis=0, tiled=True)  23.1 us
    all_gather x1, blocking collectives, local(): lax.all_gather(own_docs, 'cp', axis=0, tiled=True)  20.4 us
    all_to_all x1, waiting for transfers between devices, summed_on_arrival(): lax.all_to_all(blocks, axis, split_axis=0, concat_axis=0, tiled=True)  18 us
    dot_general x1, matrix products, expert_hidden(): gated = jnp.dot(rows_in, gate_weight[0], preferred_element_type=jnp.float32)  9.37 us
    dot_general x1, matrix products, local(): jnp.dot(rows_in, down_weight[0], preferred_element_type=jnp.float32)  7.79 us
  transfers between devices with their start and end apart: 5, of which 4 were waited for; matrix products, arithmetic and copies ran while one was open for 2% of the time, Pallas kernels for 0%

commit v1 on v0

--- a/solution.py
+++ b/solution.py
@@ -119,7 +119,9 @@
     ).astype(jnp.bfloat16)
     projected = jnp.dot(attended, out_weight, preferred_element_type=jnp.float32)
     quarter_width = residual.shape[1] // ep_count
-    summed = lax.psum(projected.astype(jnp.bfloat16), "ep").astype(jnp.float32)
+    summed = jnp.sum(lax.all_gather(projected.astype(jnp.bfloat16), "ep"), axis=0).astype(
+        jnp.float32
+    )
     hidden_full = (residual.astype(jnp.float32) + summed).astype(jnp.bfloat16)
     hidden_state = lax.dynamic_slice_in_dim(hidden_full, ep_rank * quarter_width, quarter_width, 1)
     values_wide = hidden_full.astype(jnp.float32)

time: 388 us -> 410 us (1.057)
  waiting for transfers between devices: 250 us -> 266 us
  other arithmetic: 21.3 us -> 26.8 us
    all_gather x0 -> x1, waiting for transfers between devices: none -> 64.7 us  [local(): lax.all_gather(projected.astype(jnp.bfloat16), 'ep')]
    psum x1 -> x0, waiting for transfers between devices: 49.7 us -> none  [local(): summed = lax.psum(projected.astype(jnp.bfloat16), 'ep').astype(jnp.float32)]
    reduce_sum x0 -> x1, other arithmetic: none -> 5.53 us  [local(): jnp.sum(lax.all_gather(projected.astype(jnp.bfloat16), 'ep'), axis=0)]
where the time goes in v1:
time: 410 us; the launch traced here: 409 us
  waiting for transfers between devices  266 us (65%)
  blocking collectives  43.5 us (11%)
  matrix products  37 us (9%)
  other arithmetic  26.8 us (7%)
  local copies, waits for them, and re-layouts  16.2 us (4%)
  between operations  15.2 us (4%)
  starting transfers between devices  4.68 us (1%)
    reduce_scatter x1, waiting for transfers between devices, local(): lax.psum_scatter(jnp.dot(rows_in, down_weight[0], preferred_element_type=...  112 us
    all_gather x1, waiting for transfers between devices, local(): lax.all_gather(packed, 'cp', axis=0, tiled=True)  71.1 us
    all_gather x1, waiting for transfers between devices, local(): lax.all_gather(projected.astype(jnp.bfloat16), 'ep')  64.7 us
    all_gather x1, blocking collectives, local(): lax.all_gather(own_pos, 'cp', axis=0, tiled=True)  23.1 us
    all_gather x1, blocking collectives, local(): lax.all_gather(own_docs, 'cp', axis=0, tiled=True)  20.4 us
    all_to_all x1, waiting for transfers between devices, summed_on_arrival(): lax.all_to_all(blocks, axis, split_axis=0, concat_axis=0, tiled=True)  18 us
    dot_general x1, matrix products, expert_hidden(): gated = jnp.dot(rows_in, gate_weight[0], preferred_element_type=jnp.float32)  9.37 us
  transfers between devices with their start and end apart: 5, of which 4 were waited for; matrix products, arithmetic and copies ran while one was open for 2% of the time, Pallas kernels for 0%

profile of v1, /device:TPU:0, one launch (start us, length us, event | category | flops | bytes accessed | tf_op | source)
XLA Modules:
  0.0 409.2 jit_solution(3724546682244724444)
XLA Ops:
  7.2 1.6 pad_maximum_fusion
  11.5 23.1 %all-gather.2 = s32[32,1,128]{2,1,0:T(1,128)S(1)} all-gather(s32[1,1,128]{2,1,0:T(1,128)S(1)} %fusion.40), channel_id=1, replica_groups=mesh['cp'=32,'ep'=4] {'cp'}, dimensions={0}, use_global_device_ids=true | all-gather | bytes 16896 | tf_op jit(solution)/shard_map/all_gather | solution.py:104
  35.4 20.4 %all-gather.1 = s32[32,1,128]{2,1,0:T(1,128)S(1)} all-gather(s32[1,1,128]{2,1,0:T(1,128)S(1)} %dynamic-slice_bitcast_fusion), channel_id=1, replica_groups=mesh['cp'=32,'ep'=4] {'cp'}, dimensions={0}, use_global_device_ids=true | all-gather | bytes 16896 | tf_op jit(solution)/shard_map/all_gather | solution.py:103
  58.4 15.5 %conditional.1 = (f32[128,6]{0,1:T(8,128)}, f32[128,6,128]{0,2,1:T(8,128)S(1)}) conditional(s32[]{:T(128)} %convert_element_type.66, () %tuple.16, (s32[4096]{0:T(1024)}, s32[128]{0:T(128)}, s32[4096]{0:T(1024)S(1)}, s32[128]{0:T(128)}, bf16[128,768]{1,0:T(8,128)(2,1)}, /*index=5*/bf16[4096,256]{1,0:T(8,128)(2,1)}) %tuple.42), branch_computations={%region_1.0_spmd, %region_2.5_spmd} | conditional | flops 1653079296 | bytes 53465160 | solution.py:110
  58.4 2.0 compare_and_fusion
  61.5 3.9 fusion
  65.5 4.7 %fusion.2 = f32[128,6]{0,1:T(8,128)} fusion(f32[128,6,4096]{2,0,1:T(8,128)S(1)} %get-tuple-element.61, f32[128,6]{0,1:T(8,128)S(1)} %broadcast_maximum_fusion, pred[128,4096]{1,0:T(8,128)(4,1)S(1)} %copy-done.1), kind=kLoop, calls=%fused_computation.5 | loop fusion | flops 15727872 | bytes 13113344 | tf_op jit(solution)/shard_map/cond/branch_1_fun/reduce_sum | solution.py:81
  70.2 3.6 fusion.3
  74.6 6.3 %convolution_convert_fusion.1 = bf16[128,6144]{1,0:T(8,128)(2,1)} fusion(bf16[128,768]{0,1:T(8,128)(2,1)S(1)} %bitcast.59, bf16[768,6144]{1,0:T(8,128)(2,1)} %param.19), kind=kOutput, calls=%fused_computation.19 | convolution fusion | flops 1208745984 | bytes 11206656 | tf_op jit(solution)/shard_map/dot_general | solution.py:120
  81.5 64.7 %all-gather.11.cloned.1.call-done = bf16[512,6144]{1,0:T(8,128)(2,1)} async-done(((bf16[128,6144]{1,0:T(8,128)(2,1)}), bf16[512,6144]{1,0:T(8,128)(2,1)}) %all-gather.11.cloned.1.call-update) | async-done | bytes 6291472 | tf_op jit(solution)/shard_map/all_gather | solution.py:122
  146.2 5.5 %reduce_sum.42 = bf16[128,6144]{1,0:T(8,128)(2,1)} reduce(bf16[4,128,6144]{2,1,0:T(8,128)(2,1)} %bitcast.58, bf16[]{:T(256)} %constant.37.clone.1), dimensions={0}, to_apply=%region_5.6 | reduce | flops 2359296 | bytes 7864322 | tf_op jit(solution)/shard_map/reduce_sum | solution.py:122
  151.7 2.6 fusion.14
  157.0 71.1 %all-gather.9.cloned.1.call-done = bf16[1280,6144]{1,0:T(8,128)(2,1)} async-done(((bf16[40,6144]{1,0:T(8,128)(2,1)}), bf16[1280,6144]{1,0:T(8,128)(2,1)}) %all-gather.9.cloned.1.call-update) | async-done | bytes 15728656 | tf_op jit(solution)/shard_map/all_gather | solution.py:145
  228.1 9.4 %fusion.22 = f32[1280,256]{1,0:T(8,128)S(1)} fusion(bf16[1280,6144]{1,0:T(8,128)(2,1)} %all-gather.9.cloned.1.call-done, bf16[1,6144,256]{2,1,0:T(8,128)(2,1)} %param.25), kind=kOutput, calls=%fused_computation.32 | convolution fusion | flops 4026531840 | bytes 20185088 | tf_op jit(solution)/shard_map/dot_general | solution.py:34
  239.8 4.6 %fusion.27 = bf16[1280,256]{1,0:T(8,128)(2,1)S(1)} fusion(bf16[1280,6144]{1,0:T(8,128)(2,1)S(1)} %copy-done.9, bf16[1,6144,256]{2,1,0:T(8,128)(2,1)S(1)} %copy-done.10, f32[1280,256]{1,0:T(8,128)S(1)} %fusion.22), kind=kOutput, calls=%fused_computation.36 | convolution fusion | flops 4028497920 | bytes 20840448 | tf_op jit(solution)/shard_map/dot_general | solution.py:35
  244.4 7.8 %convolution_convert_fusion = bf16[1280,6144]{1,0:T(8,128)(2,1)} fusion(bf16[1280,256]{1,0:T(8,128)(2,1)S(1)} %fusion.27, bf16[1,256,6144]{2,1,0:T(8,128)(2,1)S(1)} %copy-done), kind=kOutput, calls=%fused_computation.18 | convolution fusion | flops 4034396160 | bytes 19529728 | tf_op jit(solution)/shard_map/dot_general | solution.py:148
  252.9 111.8 %reduce-scatter.2.cloned.1.call-done = bf16[40,6144]{1,0:T(8,128)(2,1)} async-done(((bf16[1280,6144]{1,0:T(8,128)(2,1)}), bf16[40,6144]{1,0:T(8,128)(2,1)}) %reduce-scatter.2.cloned.1.call-update) | async-done | bytes 491536 | tf_op jit(solution)/shard_map/reduce_scatter | solution.py:147
  364.8 2.1 convert_element_type.78
  366.8 5.7 %gather_fusion = f32[128,6144]{1,0:T(8,128)} fusion(f32[40,6144]{1,0:T(8,128)} %convert_element_type.78, s32[1024]{0:T(1024)S(1)} %pad_clamp_fusion), kind=kCustom, calls=%fused_computation | custom fusion | bytes 6291968 | tf_op jit(solution)/shard_map/jit(_take)/gather | solution.py:153
  372.5 3.5 fusion.30
  376.0 4.3 %all-to-all-start = ((bf16[4,128,1536]{2,1,0:T(8,128)(2,1)}), bf16[4,128,1536]{2,1,0:T(8,128)(2,1)}, u32[]{:S(2)}, u32[]{:S(2)}) async-start(bf16[4,128,1536]{2,1,0:T(8,128)(2,1)} %fusion.30), calls=%async_computation.1 | async-start | bytes 3145728 | tf_op jit(solution)/shard_map/all_to_all | solution.py:29
  380.4 1.8 constant_dynamic-slice_fusion
  382.1 18.0 %all-to-all-done = bf16[4,128,1536]{2,1,0:T(8,128)(2,1)} async-done(((bf16[4,128,1536]{2,1,0:T(8,128)(2,1)}), bf16[4,128,1536]{2,1,0:T(8,128)(2,1)}, u32[]{:S(2)}, u32[]{:S(2)}) %all-to-all-start) | async-done | bytes 1572896 | tf_op jit(solution)/shard_map/all_to_all | solution.py:29
  400.2 2.5 reduce_sum.44
  (52 shorter events, 12.9 us)
Async XLA Ops:
  7.2 237.3 %copy-start = (bf16[1,256,6144]{2,1,0:T(8,128)(2,1)S(1)}, bf16[1,256,6144]{2,1,0:T(8,128)(2,1)}, u32[]{:S(2)}) copy-start(bf16[1,256,6144]{2,1,0:T(8,128)(2,1)} %param.27) | copy-start | bytes 9437188
  7.2 51.2 %all-gather.7.cloned.1.call-start = ((), (), s32[]{:S(2)}) async-start(), calls=%async_computation.2 | async-start | bytes 2162688 | tf_op jit(solution)/shard_map/all_gather | solution.py:15
  8.8 137.3 %all-gather.11.cloned.1.call-start = ((), (), s32[]{:S(2)}) async-start(), calls=%async_computation.5 | async-start | bytes 7864320 | tf_op jit(solution)/shard_map/all_gather | solution.py:122
  11.5 44.2 %copy-start.6 = (s32[128]{0:T(128)}, s32[128]{0:T(128)S(1)}, u32[]{:S(2)}) copy-start(s32[128]{0:T(128)S(1)} %dynamic_slice.10) | copy-start | bytes 1540
  55.8 0.6 copy-start.4
  55.8 0.6 copy-start.7
  61.5 4.0 copy-start.1
  65.4 4.8 %copy-start.3 = (bf16[4096,256]{1,0:T(8,128)(2,1)S(1)}, bf16[4096,256]{1,0:T(8,128)(2,1)}, u32[]{:S(2)}) copy-start(bf16[4096,256]{1,0:T(8,128)(2,1)} %get-tuple-element.20) | copy-start | bytes 6291460 | tf_op jit(solution)/shard_map/cond
  74.5 6.5 %copy-start.5 = (s32[128,2]{0,1:T(2,128)S(1)}, s32[128,2]{0,1:T(2,128)}, u32[]{:S(2)}) copy-start(s32[128,2]{0,1:T(2,128)} %param.23) | copy-start | bytes 3076
  80.9 147.2 %all-gather.9.cloned.1.call-start = ((), (), s32[]{:S(2)}) async-start(), calls=%async_computation.3 | async-start | bytes 16220160 | tf_op jit(solution)/shard_map/all_gather | solution.py:145
  151.7 3.8 copy-start.11
  154.3 1.1 copy-start.2
  156.9 207.8 %reduce-scatter.2.cloned.1.call-start = ((), (), s32[]{:S(2)}) async-start(), calls=%async_computation.4 | async-start | bytes 16220160 | tf_op jit(solution)/shard_map/reduce_scatter | solution.py:147
  228.1 10.8 %copy-start.9 = (bf16[1280,6144]{1,0:T(8,128)(2,1)S(1)}, bf16[1280,6144]{1,0:T(8,128)(2,1)}, u32[]{:S(2)}) copy-start(bf16[1280,6144]{1,0:T(8,128)(2,1)} %all-gather.9.cloned.1.call-done) | copy-start | bytes 47185924
  228.1 11.7 %copy-start.10 = (bf16[1,6144,256]{2,1,0:T(8,128)(2,1)S(1)}, bf16[1,6144,256]{2,1,0:T(8,128)(2,1)}, u32[]{:S(2)}) copy-start(bf16[1,6144,256]{2,1,0:T(8,128)(2,1)} %param.26) | copy-start | bytes 9437188
  252.2 0.7 copy-start.8
  376.0 24.2 %all-to-all-start = ((bf16[4,128,1536]{2,1,0:T(8,128)(2,1)}), bf16[4,128,1536]{2,1,0:T(8,128)(2,1)}, u32[]{:S(2)}, u32[]{:S(2)}) async-start(bf16[4,128,1536]{2,1,0:T(8,128)(2,1)} %fusion.30), calls=%async_computation.1 | async-start | bytes 3145728 | tf_op jit(solution)/shard_map/all_to_all | solution.py:29
Sparse Core Ops, SparseCore 0:
  10.8 46.2 all-gather.6
  81.0 65.1 all-gather.10
  157.1 70.9 all-gather.8
  252.4 112.3 reduce-scatter.1
